TPU v7x, 32 devices: a whole 2x2x4 slice. The times are simulated.
32 devices in a mesh: gx: 4 (over x, core), gy: 8 (over z, y).
Axes of the slice: x: 2, y: 2, z: 4, core: 2. Of those that a mesh axis runs over, the one named last changes fastest.
Arguments:
- right_side: float32 [2, 64, 256, 128], P(None, 'gx', 'gy'), may hold values from -6 to 6
- wavenumber: float32 [64, 256, 128], P('gx', 'gy'), may hold values from 0.2 to 1
- pml_layer: int32 [64, 256, 128], P('gx', 'gy'), may hold values from 0 to 3
- aggregate: int32 [64, 256, 128], P('gx', 'gy'), may hold values from 0 to 15, as said below
- coarse_inverse: float32 [2, 512, 512], P(None, ('gx', 'gy')), may hold values from -0.0029296875 to 0.0029296875
Outputs:
- solution: float32 [2, 64, 256, 128], P(None, 'gx', 'gy')
- hessenberg: float32 [2, 5, 4], replicated
Inputs may be any that keep to these rules, and one draw needn't show every extreme that they name: `aggregate`: along the third dimension the value never falls, and every value of 0 to 15 occurs in every column of cells.
All inputs are finite; a program needn't handle non-finite values.
Results may differ from a plain program's by a relative error of at most 0.00015.
Values sent between devices are 32-bit elements; how exact they have to be, the bound alone decides.
No kernel may reach another device: no remote copies, remote signals or barrier semaphores. Data moves between devices by JAX's collectives and lax.ppermute only.
A program may use at most 64 MiB of HBM per device.

v0:
```python
import math
import jax
import jax.numpy as jnp
from jax import lax
from jax.sharding import PartitionSpec as P

ITERS = 4
damping = 0.8
pml_strength = 3.0
epsilon = 1e-06


def with_halo(block, sides, width):
    for axis, dim in sides:
        count = lax.axis_size(axis)
        forward = [(i, i + 1) for i in range(count - 1)]
        backward = [(target, source) for source, target in forward]
        low = lax.ppermute(
            lax.slice_in_dim(block, block.shape[dim] - width, None, axis=dim), axis, forward
        )
        high = lax.ppermute(lax.slice_in_dim(block, 0, width, axis=dim), axis, backward)
        block = jnp.concatenate([low, block, high], axis=dim)
    return block


def coefficients(wavenumber, layer_float):
    wave_sq = wavenumber * wavenumber
    depth = layer_float / 3.0
    absorb = wave_sq * (pml_strength * depth * depth)
    diag_re = 6.0 - wave_sq
    magnitude = diag_re * diag_re + absorb * absorb
    return (wave_sq, absorb, damping * diag_re / magnitude, damping * absorb / magnitude)


def operate_inner(extended, wave_sq, absorb):
    middle = extended[:, 1:-1, 1:-1]
    above = jnp.concatenate([middle[..., 1:], jnp.zeros_like(middle[..., :1])], -1)
    below = jnp.concatenate([jnp.zeros_like(middle[..., :1]), middle[..., :-1]], -1)
    beside = (
        extended[:, 2:, 1:-1]
        + extended[:, :-2, 1:-1]
        + extended[:, 1:-1, 2:]
        + extended[:, 1:-1, :-2]
        + above
        + below
    )
    real_part = (6.0 - wave_sq) * middle[0] - beside[0] + absorb * middle[1]
    imag_part = (6.0 - wave_sq) * middle[1] - beside[1] - absorb * middle[0]
    return jnp.stack([real_part, imag_part])


def smooth(field, scale_re, scale_im):
    return jnp.stack(
        [scale_re * field[0] - scale_im * field[1], scale_re * field[1] + scale_im * field[0]]
    )


def complex_scale(scale_re, scale_im, field):
    return jnp.stack(
        [scale_re * field[0] - scale_im * field[1], scale_re * field[1] + scale_im * field[0]]
    )


def inner_local(left, right):
    return jnp.stack(
        [
            jnp.sum(left[0] * right[0] + left[1] * right[1]),
            jnp.sum(left[0] * right[1] - left[1] * right[0]),
        ]
    )


def least_squares(hessenberg, beta):
    real_h = hessenberg[0]
    imag_h = hessenberg[1]
    stacked = jnp.concatenate(
        [jnp.concatenate([real_h, -imag_h], 1), jnp.concatenate([imag_h, real_h], 1)], 0
    )
    count = stacked.shape[1]
    target = jnp.zeros((stacked.shape[0],), jnp.float32).at[0].set(beta)
    ortho = []
    upper = {}
    for column in range(count):
        vector = stacked[:, column]
        for position in range(column):
            upper[position, column] = jnp.zeros((), jnp.float32)
        for repeat in range(2):
            for position in range(len(ortho)):
                weight = jnp.sum(ortho[position] * vector)
                vector = vector - weight * ortho[position]
                upper[position, column] = upper[position, column] + weight
        norm_value = jnp.sqrt(jnp.sum(vector * vector))
        upper[column, column] = norm_value
        ortho.append(vector / norm_value)
    project = [jnp.sum(basis_vec * target) for basis_vec in ortho]
    solved = [None] * count
    for column in reversed(range(count)):
        total = project[column]
        for later in range(column + 1, count):
            total = total - upper[column, later] * solved[later]
        solved[column] = total / upper[column, column]
    return solved


def restrict(flat_field, flat_ids, levels_count):
    total = flat_ids.shape[0]
    block = math.gcd(total, 16384)
    levels = jnp.arange(levels_count, dtype=jnp.int32)

    def accumulate(step_index, result):
        piece = lax.dynamic_slice_in_dim(flat_field, step_index * block, block, 1)
        labels = lax.dynamic_slice_in_dim(flat_ids, step_index * block, block, 0)
        onehot = (labels[None, :] == levels[:, None]).astype(jnp.float32)
        return result + lax.dot_general(
            piece, onehot, (((1,), (1,)), ((), ())), precision=lax.Precision.HIGHEST
        )

    return lax.fori_loop(0, total // block, accumulate, jnp.zeros((2, levels_count), jnp.float32))


def prolong(values, flat_ids):
    total = flat_ids.shape[0]
    block = math.gcd(total, 16384)
    levels = jnp.arange(values.shape[1], dtype=jnp.int32)

    def place(step_index, result):
        labels = lax.dynamic_slice_in_dim(flat_ids, step_index * block, block, 0)
        onehot = (levels[:, None] == labels[None, :]).astype(jnp.float32)
        piece = jnp.dot(values, onehot, precision=lax.Precision.HIGHEST)
        return lax.dynamic_update_slice_in_dim(result, piece, step_index * block, 1)

    return lax.fori_loop(0, total // block, place, jnp.zeros((2, total), jnp.float32))


def coarse_fix(remainder, flat_ids, coarse_inverse):
    highest = lax.Precision.HIGHEST
    levels_count = coarse_inverse.shape[1]
    total_coarse = coarse_inverse.shape[2]
    partial_value = restrict(remainder.reshape(2, -1), flat_ids, levels_count)
    offset = (lax.axis_index("gx") * lax.axis_size("gy") + lax.axis_index("gy")) * levels_count
    padded = lax.dynamic_update_slice(
        jnp.zeros((2, total_coarse), jnp.float32), partial_value, (jnp.zeros((), jnp.int32), offset)
    )
    whole = lax.psum(padded, ("gx", "gy"))
    own_re = jnp.dot(coarse_inverse[0], whole[0], precision=highest) - jnp.dot(
        coarse_inverse[1], whole[1], precision=highest
    )
    own_im = jnp.dot(coarse_inverse[0], whole[1], precision=highest) + jnp.dot(
        coarse_inverse[1], whole[0], precision=highest
    )
    return prolong(jnp.stack([own_re, own_im]), flat_ids).reshape(remainder.shape)


def operate_near(field, wave_sq, absorb):
    extended = with_halo(field, (("gx", 1), ("gy", 2)), 1)
    return operate_inner(extended, wave_sq, absorb)


def operate_final(field, wave_sq, absorb):
    extended = with_halo(field, (("gx", 1), ("gy", 2)), 1)
    return operate_inner(extended, wave_sq, absorb)


def body(right_side, wavenumber, pml_layer, aggregate, coarse_inverse):
    layer_float = pml_layer.astype(jnp.float32)
    wave_sq, absorb, scale_re, scale_im = coefficients(wavenumber, layer_float)
    flat_ids = aggregate.reshape(-1)
    beta = jnp.sqrt(lax.psum(jnp.sum(right_side * right_side), ("gx", "gy")) + epsilon)
    basis = [right_side / beta]
    directions = []
    columns_re = []
    columns_im = []
    for column in range(ITERS):
        vector = basis[column]
        first = smooth(vector, scale_re, scale_im)
        second = first + smooth(vector - operate_near(first, wave_sq, absorb), scale_re, scale_im)
        remainder = vector - operate_near(second, wave_sq, absorb)
        direction = second + coarse_fix(remainder, flat_ids, coarse_inverse)
        image = operate_final(direction, wave_sq, absorb)
        local_dots = jnp.stack([inner_local(member, image) for member in basis], 1)
        dots, squared = lax.psum((local_dots, jnp.sum(image * image)), ("gx", "gy"))
        for position in range(len(basis)):
            image = image - complex_scale(dots[0, position], dots[1, position], basis[position])
        leftover = squared - jnp.sum(dots * dots)
        length = jnp.sqrt(jnp.maximum(leftover, 0.0) + epsilon)
        tail = jnp.zeros((ITERS - 1 - column,), jnp.float32)
        columns_re.append(jnp.concatenate([dots[0], length[None], tail]))
        columns_im.append(jnp.concatenate([dots[1], jnp.zeros((1,), jnp.float32), tail]))
        directions.append(direction)
        if column + 1 < ITERS:
            basis.append(image / length)
    hessenberg = jnp.stack([jnp.stack(columns_re, 1), jnp.stack(columns_im, 1)])
    solved = least_squares(hessenberg, beta)
    solution = jnp.zeros_like(right_side)
    for column in range(ITERS):
        solution = solution + complex_scale(
            solved[column], solved[ITERS + column], directions[column]
        )
    return (solution, hessenberg)


def solution(mesh):
    return jax.shard_map(
        body,
        mesh=mesh,
        in_specs=(
            P(None, "gx", "gy", None),
            P("gx", "gy", None),
            P("gx", "gy", None),
            P("gx", "gy", None),
            P(None, ("gx", "gy"), None),
        ),
        out_specs=(P(None, "gx", "gy", None), P()),
        check_vma=False,
    )
```

profile of v0, /device:TPU:0, one launch (start us, length us, event | category | flops | bytes accessed | tf_op | source)
XLA Modules:
  0.0 809.6 jit_solution(285482413600228902)
XLA Ops:
  2.5 42.2 %psum.91 = f32[]{:T(128)} all-reduce(f32[]{:T(128)} %multiply_reduce_fusion.3), channel_id=1, replica_groups=mesh['gx'=4,'gy'=8] {'gx','gy'}, use_global_device_ids=true, to_apply=%region_1.0 | all-reduce | flops 1 | bytes 8 | tf_op jit(solution)/shard_map/psum | solution.py:168
  48.0 3.0 collective-permute-start.1
  53.2 5.0 collective-permute-start.3
  62.3 3.0 collective-permute-start.5
  67.5 5.4 collective-permute-start.7
  76.2 7.0 while.117
  83.3 46.5 %psum.92 = f32[2,512]{1,0:T(2,128)S(1)} all-reduce(f32[2,512]{1,0:T(2,128)S(1)} %dynamic_update_slice.40), channel_id=1, replica_groups=mesh['gx'=4,'gy'=8] {'gx','gy'}, use_global_device_ids=true, to_apply=%region_4.0 | all-reduce | flops 1024 | bytes 8192 | tf_op jit(solution)/shard_map/psum | solution.py:144
  130.6 2.0 while.113
  134.9 3.0 collective-permute-start.9
  140.2 4.8 collective-permute-start.11
  149.7 43.8 %all-reduce.29 = (f32[2,1]{0,1:T(1,128)S(1)}, f32[]{:T(128)}) all-reduce(f32[2,1]{0,1:T(1,128)S(1)} %maximum_bitcast_fusion.1, f32[]{:T(128)} %multiply_reduce_fusion.2), channel_id=1, replica_groups=mesh['gx'=4,'gy'=8] {'gx','gy'}, use_global_device_ids=true, to_apply=%region_9.0 | all-reduce | flops 3 | bytes 24 | tf_op jit(solution)/shard_map/psum | solution.py:181
  199.2 3.0 collective-permute-start.13
  204.4 5.0 collective-permute-start.15
  214.4 3.4 collective-permute-start.17
  220.2 5.6 collective-permute-start.19
  228.3 2.1 divide_subtract_fusion.2
  230.3 6.9 while.118
  237.5 47.6 %psum.95 = f32[2,512]{1,0:T(2,128)S(1)} all-reduce(f32[2,512]{1,0:T(2,128)S(1)} %dynamic_update_slice.41), channel_id=1, replica_groups=mesh['gx'=4,'gy'=8] {'gx','gy'}, use_global_device_ids=true, to_apply=%region_15.0 | all-reduce | flops 1024 | bytes 8192 | tf_op jit(solution)/shard_map/psum | solution.py:144
  285.9 2.0 while.114
  290.5 3.0 collective-permute-start.21
  295.7 4.8 collective-permute-start.23
  306.9 43.6 %all-reduce.28 = (f32[2,2]{0,1:T(2,128)S(1)}, f32[]{:T(128)}) all-reduce(f32[2,2]{0,1:T(2,128)S(1)} %pad_maximum_fusion.166, f32[]{:T(128)} %multiply_reduce_fusion.1), channel_id=1, replica_groups=mesh['gx'=4,'gy'=8] {'gx','gy'}, use_global_device_ids=true, to_apply=%region_22.0 | all-reduce | flops 5 | bytes 40 | tf_op jit(solution)/shard_map/psum | solution.py:181
  357.4 3.0 collective-permute-start.25
  362.6 5.0 collective-permute-start.27
  372.0 3.3 collective-permute-start.29
  377.5 5.3 collective-permute-start.31
  385.8 2.4 divide_subtract_fusion.1
  388.2 6.9 while.119
  395.3 47.6 %psum.98 = f32[2,512]{1,0:T(2,128)S(1)} all-reduce(f32[2,512]{1,0:T(2,128)S(1)} %dynamic_update_slice.42), channel_id=1, replica_groups=mesh['gx'=4,'gy'=8] {'gx','gy'}, use_global_device_ids=true, to_apply=%region_28.0 | all-reduce | flops 1024 | bytes 8192 | tf_op jit(solution)/shard_map/psum | solution.py:144
  443.7 2.0 while.115
  448.4 3.0 collective-permute-start.33
  453.6 4.8 collective-permute-start.35
  467.3 43.7 %all-reduce.27 = (f32[2,3]{0,1:T(4,128)S(1)}, f32[]{:T(128)}) all-reduce(f32[2,3]{0,1:T(4,128)S(1)} %pad_maximum_fusion.161, f32[]{:T(128)} %multiply_reduce_fusion), channel_id=1, replica_groups=mesh['gx'=4,'gy'=8] {'gx','gy'}, use_global_device_ids=true, to_apply=%region_37.0 | all-reduce | flops 7 | bytes 56 | tf_op jit(solution)/shard_map/psum | solution.py:181
  513.7 2.5 multiply_subtract_fusion.5
  522.2 3.0 collective-permute-start.37
  528.0 5.1 collective-permute-start.39
  537.5 3.1 collective-permute-start.41
  542.8 5.5 collective-permute-start.43
  550.0 2.8 divide_subtract_fusion
  552.9 6.9 while.120
  560.0 47.0 %psum.101 = f32[2,512]{1,0:T(2,128)S(1)} all-reduce(f32[2,512]{1,0:T(2,128)S(1)} %dynamic_update_slice.43), channel_id=1, replica_groups=mesh['gx'=4,'gy'=8] {'gx','gy'}, use_global_device_ids=true, to_apply=%region_43.0 | all-reduce | flops 1024 | bytes 8192 | tf_op jit(solution)/shard_map/psum | solution.py:144
  608.5 4.3 while.116
  615.6 3.0 collective-permute-start.45
  620.8 4.8 collective-permute-start.47
  636.3 43.7 %all-reduce.26 = (f32[2,4]{0,1:T(4,128)S(1)}, f32[]{:T(128)}) all-reduce(f32[2,4]{0,1:T(4,128)S(1)} %pad_maximum_fusion.162, f32[]{:T(128)} %fusion.133), channel_id=1, replica_groups=mesh['gx'=4,'gy'=8] {'gx','gy'}, use_global_device_ids=true, to_apply=%region_54.0 | all-reduce | flops 9 | bytes 72 | tf_op jit(solution)/shard_map/psum | solution.py:181
  685.7 1.9 multiply_reduce_fusion.61
  689.7 2.0 fusion.293
  691.7 2.0 multiply_reduce_fusion.55
  693.6 1.9 multiply_reduce_fusion.57
  705.4 1.9 multiply_reduce_fusion.47
  708.7 2.6 multiply_reduce_fusion.41
  711.3 2.0 multiply_reduce_fusion.40
  715.1 2.6 multiply_reduce_fusion.39
  718.3 1.9 multiply_reduce_fusion.38
  720.3 2.0 fusion.299
  724.1 1.9 multiply_reduce_fusion.30
  725.9 3.1 multiply_reduce_fusion.29
  733.3 1.9 multiply_reduce_fusion.27
  736.5 2.6 multiply_reduce_fusion.19
  740.9 3.1 multiply_reduce_fusion.17
  749.0 2.6 multiply_reduce_fusion.15
  752.3 1.9 multiply_reduce_fusion.14
  758.7 2.0 multiply_reduce_fusion.11
  766.4 1.9 multiply_reduce_fusion.7
  (474 shorter events, 198.6 us)
Async XLA Ops:
  0.6 44.7 %copy-start.23 = (f32[2,16,32,128]{3,2,1,0:T(8,128)S(1)}, f32[2,16,32,128]{3,2,1,0:T(8,128)}, u32[]{:S(2)}) copy-start(f32[2,16,32,128]{3,2,1,0:T(8,128)} %param.23) | copy-start | bytes 1572868
  46.6 323.2 %copy-start.6 = (f32[16,32,128]{2,1,0:T(8,128)}, f32[16,32,128]{2,1,0:T(8,128)S(1)}, u32[]{:S(2)}) copy-start(f32[16,32,128]{2,1,0:T(8,128)S(1)} %get-tuple-element.1108) | copy-start | bytes 786436
  46.7 4.3 collective-permute-start
  48.0 3.9 collective-permute-start.1
  51.9 6.5 collective-permute-start.2
  53.2 6.5 collective-permute-start.3
  61.0 4.3 collective-permute-start.4
  62.3 3.9 collective-permute-start.5
  66.2 7.0 collective-permute-start.6
  67.5 6.9 collective-permute-start.7
  76.2 53.6 %copy-start.40 = (f32[2,16,512]{2,1,0:T(8,128)S(1)}, f32[2,16,512]{2,1,0:T(8,128)}, u32[]{:S(2)}) copy-start(f32[2,16,512]{2,1,0:T(8,128)} %param.27) | copy-start | bytes 196612
  133.6 4.3 collective-permute-start.8
  134.9 3.9 collective-permute-start.9
  138.9 6.3 collective-permute-start.10
  140.2 6.3 collective-permute-start.11
  147.6 63.7 %copy-start.24 = (f32[16,32,128]{2,1,0:T(8,128)}, f32[16,32,128]{2,1,0:T(8,128)S(1)}, u32[]{:S(2)}) copy-start(f32[16,32,128]{2,1,0:T(8,128)S(1)} %get-tuple-element.1104) | copy-start | bytes 786436
  147.6 63.7 %copy-start.26 = (f32[16,32,128]{2,1,0:T(8,128)}, f32[16,32,128]{2,1,0:T(8,128)S(1)}, u32[]{:S(2)}) copy-start(f32[16,32,128]{2,1,0:T(8,128)S(1)} %get-tuple-element.1105) | copy-start | bytes 786436
  197.8 155.2 %copy-start.2 = (f32[2,16,32,128]{3,2,1,0:T(8,128)}, f32[2,16,32,128]{3,2,1,0:T(8,128)S(1)}, u32[]{:S(2)}) copy-start(f32[2,16,32,128]{3,2,1,0:T(8,128)S(1)} %fusion.124) | copy-start | bytes 1572868
  197.9 13.8 %copy-start.16 = (f32[16,32,128]{2,1,0:T(8,128)}, f32[16,32,128]{2,1,0:T(8,128)S(1)}, u32[]{:S(2)}) copy-start(f32[16,32,128]{2,1,0:T(8,128)S(1)} %get-tuple-element.1136) | copy-start | bytes 786436
  197.9 13.8 %copy-start.18 = (f32[16,32,128]{2,1,0:T(8,128)}, f32[16,32,128]{2,1,0:T(8,128)S(1)}, u32[]{:S(2)}) copy-start(f32[16,32,128]{2,1,0:T(8,128)S(1)} %get-tuple-element.1137) | copy-start | bytes 786436
  197.9 4.3 collective-permute-start.12
  199.2 3.9 collective-permute-start.13
  203.1 6.5 collective-permute-start.14
  204.4 6.4 collective-permute-start.15
  213.1 4.7 collective-permute-start.16
  214.4 4.5 collective-permute-start.17
  218.9 7.1 collective-permute-start.18
  220.2 6.6 collective-permute-start.19
  289.2 4.3 collective-permute-start.20
  290.5 3.9 collective-permute-start.21
  294.4 6.3 collective-permute-start.22
  295.7 6.3 collective-permute-start.23
  354.3 15.2 %copy-start.45 = (f32[1,16,32,128]{3,2,1,0:T(8,128)}, f32[1,16,32,128]{3,2,1,0:T(8,128)S(1)}, u32[]{:S(2)}) copy-start(f32[1,16,32,128]{3,2,1,0:T(8,128)S(1)} %get-tuple-element.1202) | copy-start | bytes 786436
  354.3 15.2 %copy-start.47 = (f32[1,16,32,128]{3,2,1,0:T(8,128)}, f32[1,16,32,128]{3,2,1,0:T(8,128)S(1)}, u32[]{:S(2)}) copy-start(f32[1,16,32,128]{3,2,1,0:T(8,128)S(1)} %get-tuple-element.1203) | copy-start | bytes 786436
  355.8 13.8 %copy-start.49 = (f32[1,16,32,128]{3,2,1,0:T(8,128)}, f32[1,16,32,128]{3,2,1,0:T(8,128)S(1)}, u32[]{:S(2)}) copy-start(f32[1,16,32,128]{3,2,1,0:T(8,128)S(1)} %get-tuple-element.1204) | copy-start | bytes 786436
  355.8 13.8 %copy-start.51 = (f32[1,16,32,128]{3,2,1,0:T(8,128)}, f32[1,16,32,128]{3,2,1,0:T(8,128)S(1)}, u32[]{:S(2)}) copy-start(f32[1,16,32,128]{3,2,1,0:T(8,128)S(1)} %get-tuple-element.1205) | copy-start | bytes 786436
  356.1 13.8 %copy-start.12 = (f32[16,32,128]{2,1,0:T(8,128)}, f32[16,32,128]{2,1,0:T(8,128)S(1)}, u32[]{:S(2)}) copy-start(f32[16,32,128]{2,1,0:T(8,128)S(1)} %get-tuple-element.1132) | copy-start | bytes 786436
  356.1 13.8 %copy-start.14 = (f32[16,32,128]{2,1,0:T(8,128)}, f32[16,32,128]{2,1,0:T(8,128)S(1)}, u32[]{:S(2)}) copy-start(f32[16,32,128]{2,1,0:T(8,128)S(1)} %get-tuple-element.1133) | copy-start | bytes 786436
  356.1 4.3 collective-permute-start.24
  357.4 3.9 collective-permute-start.25
  361.3 6.5 collective-permute-start.26
  362.6 6.4 collective-permute-start.27
  370.7 4.6 collective-permute-start.28
  372.0 4.2 collective-permute-start.29
  376.2 6.9 collective-permute-start.30
  377.5 6.6 collective-permute-start.31
  447.1 4.4 collective-permute-start.32
  448.4 3.9 collective-permute-start.33
  452.3 6.3 collective-permute-start.34
  453.6 6.3 collective-permute-start.35
  520.9 14.5 %copy-start.8 = (f32[16,32,128]{2,1,0:T(8,128)}, f32[16,32,128]{2,1,0:T(8,128)S(1)}, u32[]{:S(2)}) copy-start(f32[16,32,128]{2,1,0:T(8,128)S(1)} %get-tuple-element.1128) | copy-start | bytes 786436
  520.9 14.6 %copy-start.10 = (f32[16,32,128]{2,1,0:T(8,128)}, f32[16,32,128]{2,1,0:T(8,128)S(1)}, u32[]{:S(2)}) copy-start(f32[16,32,128]{2,1,0:T(8,128)S(1)} %get-tuple-element.1129) | copy-start | bytes 786436
  520.9 5.8 collective-permute-start.36
  522.2 4.5 collective-permute-start.37
  526.7 6.6 collective-permute-start.38
  528.0 6.5 collective-permute-start.39
  536.2 4.6 collective-permute-start.40
  537.5 4.0 collective-permute-start.41
  541.5 7.1 collective-permute-start.42
  542.8 6.8 collective-permute-start.43
  614.3 4.4 collective-permute-start.44
  615.6 3.9 collective-permute-start.45
  619.5 6.3 collective-permute-start.46
  620.8 6.3 collective-permute-start.47
  (52 other events, 92.3 us)
where the time goes:
time: 821 us; the launch traced here: 810 us
  blocking collectives  406 us (49%)
  other arithmetic  135 us (16%)
  starting transfers between devices  129 us (16%)
  between operations  54.6 us (7%)
  matrix products  39.1 us (5%)
  waiting for transfers between devices  23 us (3%)
  local copies, waits for them, and re-layouts  22.3 us (3%)
    psum x4, blocking collectives, coarse_fix(): whole = lax.psum(padded, ('gx', 'gy'))  189 us
    psum x4, blocking collectives, body(): dots, squared = lax.psum((local_dots, jnp.sum(image * image)), ('gx', 'gy'))  175 us
    ppermute x24, starting transfers between devices, with_halo(): lax.ppermute(lax.slice_in_dim(block, block.shape[dim] - width, None, axis...  98.4 us
    reduce_sum x34, other arithmetic, least_squares(): weight = jnp.sum(ortho[position] * vector)  64.5 us
    psum x1, blocking collectives, body(): lax.psum(jnp.sum(right_side * right_side), ('gx', 'gy')) + epsilon  42.2 us
    ppermute x24, starting transfers between devices, with_halo(): lax.ppermute(lax.slice_in_dim(block, 0, width, axis=dim), axis, backward)  31 us
    dot_general x16, matrix products, accumulate(): lax.dot_general(piece, onehot, (((1,), (1,)), ((), ())), precision=lax.Pr...  27.2 us
    ppermute x24, waiting for transfers between devices, with_halo(): lax.ppermute(lax.slice_in_dim(block, block.shape[dim] - width, None, axis...  22.9 us
  transfers between devices with their start and end apart: 48, of which 23 were waited for; matrix products, arithmetic and copies ran while one was open for 1% of the time, Pallas kernels for 0%

commit v1 on v0

--- a/solution.py
+++ b/solution.py
@@ -141,7 +141,7 @@
     padded = lax.dynamic_update_slice(
         jnp.zeros((2, total_coarse), jnp.float32), partial_value, (jnp.zeros((), jnp.int32), offset)
     )
-    whole = lax.psum(padded, ("gx", "gy"))
+    whole = jnp.sum(lax.all_gather(padded, ("gx", "gy")), axis=0)
     own_re = jnp.dot(coarse_inverse[0], whole[0], precision=highest) - jnp.dot(
         coarse_inverse[1], whole[1], precision=highest
     )

time: 821 us -> 913 us (1.11)
  blocking collectives: 406 us -> 498 us
    all_gather x0 -> x4, blocking collectives: none -> 285 us  [coarse_fix(): whole = jnp.sum(lax.all_gather(padded, ('gx', 'gy')), axis=0)]
    psum x4 -> x0, blocking collectives: 189 us -> none  [coarse_fix(): whole = lax.psum(padded, ('gx', 'gy'))]
  transfers between devices with their start and end apart: 48 -> 48, of which waited for: 23 -> 23; matrix products, arithmetic and copies ran while one was open for 1% -> 0% of each run, Pallas kernels for 0% -> 0%
where the time goes in v1:
time: 913 us; the launch traced here: 902 us
  blocking collectives  498 us (55%)
  other arithmetic  135 us (15%)
  starting transfers between devices  128 us (14%)
  between operations  54.6 us (6%)
  matrix products  39.1 us (4%)
  waiting for transfers between devices  23.6 us (3%)
  local copies, waits for them, and re-layouts  23.1 us (3%)
    all_gather x4, blocking collectives, coarse_fix(): whole = jnp.sum(lax.all_gather(padded, ('gx', 'gy')), axis=0)  285 us
    psum x4, blocking collectives, body(): dots, squared = lax.psum((local_dots, jnp.sum(image * image)), ('gx', 'gy'))  171 us
    ppermute x24, starting transfers between devices, with_halo(): lax.ppermute(lax.slice_in_dim(block, block.shape[dim] - width, None, axis...  96.9 us
    reduce_sum x34, other arithmetic, least_squares(): weight = jnp.sum(ortho[position] * vector)  64.5 us
    psum x1, blocking collectives, body(): lax.psum(jnp.sum(right_side * right_side), ('gx', 'gy')) + epsilon  42.2 us
    ppermute x24, starting transfers between devices, with_halo(): lax.ppermute(lax.slice_in_dim(block, 0, width, axis=dim), axis, backward)  31 us
    dot_general x16, matrix products, accumulate(): lax.dot_general(piece, onehot, (((1,), (1,)), ((), ())), precision=lax.Pr...  27.1 us
    ppermute x24, waiting for transfers between devices, with_halo(): lax.ppermute(lax.slice_in_dim(block, block.shape[dim] - width, None, axis...  23.5 us
  transfers between devices with their start and end apart: 48, of which 23 were waited for; matrix products, arithmetic and copies ran while one was open for 0% of the time, Pallas kernels for 0%

profile of v1, /device:TPU:0, one launch (start us, length us, event | category | flops | bytes accessed | tf_op | source)
XLA Modules:
  0.0 902.1 jit_solution(9483321204612995208)
XLA Ops:
  2.5 42.2 %psum.63 = f32[]{:T(128)} all-reduce(f32[]{:T(128)} %multiply_reduce_fusion.3), channel_id=1, replica_groups=mesh['gx'=4,'gy'=8] {'gx','gy'}, use_global_device_ids=true, to_apply=%region_1.0 | all-reduce | flops 1 | bytes 8 | tf_op jit(solution)/shard_map/psum | solution.py:168
  48.0 3.0 collective-permute-start.1
  53.2 5.0 collective-permute-start.3
  62.3 3.0 collective-permute-start.5
  67.5 5.4 collective-permute-start.7
  76.2 6.9 while.117
  83.3 71.8 %all_gather.28 = f32[32,2,512]{2,1,0:T(2,128)S(1)} all-gather(f32[1,2,512]{2,1,0:T(2,128)S(1)} %dynamic_update_slice.44), channel_id=1, replica_groups=mesh['gx'=4,'gy'=8] {'gx','gy'}, dimensions={0}, use_global_device_ids=true | all-gather | bytes 135168 | tf_op jit(solution)/shard_map/all_gather | solution.py:144
  156.7 2.0 while.113
  161.1 3.0 collective-permute-start.9
  166.3 4.5 collective-permute-start.11
  175.6 41.4 %all-reduce.29 = (f32[2,1]{0,1:T(1,128)S(1)}, f32[]{:T(128)}) all-reduce(f32[2,1]{0,1:T(1,128)S(1)} %maximum_bitcast_fusion.1, f32[]{:T(128)} %multiply_reduce_fusion.2), channel_id=1, replica_groups=mesh['gx'=4,'gy'=8] {'gx','gy'}, use_global_device_ids=true, to_apply=%region_9.0 | all-reduce | flops 3 | bytes 24 | tf_op jit(solution)/shard_map/psum | solution.py:181
  222.7 3.0 collective-permute-start.13
  227.9 5.0 collective-permute-start.15
  237.8 3.4 collective-permute-start.17
  243.6 5.4 collective-permute-start.19
  251.7 2.1 divide_subtract_fusion.2
  253.8 6.9 while.118
  260.9 71.4 %all_gather.30 = f32[32,2,512]{2,1,0:T(2,128)S(1)} all-gather(f32[1,2,512]{2,1,0:T(2,128)S(1)} %dynamic_update_slice.45), channel_id=1, replica_groups=mesh['gx'=4,'gy'=8] {'gx','gy'}, dimensions={0}, use_global_device_ids=true | all-gather | bytes 135168 | tf_op jit(solution)/shard_map/all_gather | solution.py:144
  333.2 2.0 while.114
  337.8 3.0 collective-permute-start.21
  343.0 4.5 collective-permute-start.23
  354.0 42.7 %all-reduce.28 = (f32[2,2]{0,1:T(2,128)S(1)}, f32[]{:T(128)}) all-reduce(f32[2,2]{0,1:T(2,128)S(1)} %pad_maximum_fusion.166, f32[]{:T(128)} %multiply_reduce_fusion.1), channel_id=1, replica_groups=mesh['gx'=4,'gy'=8] {'gx','gy'}, use_global_device_ids=true, to_apply=%region_22.0 | all-reduce | flops 5 | bytes 40 | tf_op jit(solution)/shard_map/psum | solution.py:181
  403.6 3.0 collective-permute-start.25
  408.8 5.0 collective-permute-start.27
  418.2 3.4 collective-permute-start.29
  423.8 5.2 collective-permute-start.31
  432.0 2.4 divide_subtract_fusion.1
  434.5 6.9 while.119
  441.6 71.2 %all_gather.32 = f32[32,2,512]{2,1,0:T(2,128)S(1)} all-gather(f32[1,2,512]{2,1,0:T(2,128)S(1)} %dynamic_update_slice.46), channel_id=1, replica_groups=mesh['gx'=4,'gy'=8] {'gx','gy'}, dimensions={0}, use_global_device_ids=true | all-gather | bytes 135168 | tf_op jit(solution)/shard_map/all_gather | solution.py:144
  513.7 2.0 while.115
  518.3 3.0 collective-permute-start.33
  523.5 4.5 collective-permute-start.35
  537.0 43.5 %all-reduce.27 = (f32[2,3]{0,1:T(4,128)S(1)}, f32[]{:T(128)}) all-reduce(f32[2,3]{0,1:T(4,128)S(1)} %pad_maximum_fusion.161, f32[]{:T(128)} %multiply_reduce_fusion), channel_id=1, replica_groups=mesh['gx'=4,'gy'=8] {'gx','gy'}, use_global_device_ids=true, to_apply=%region_37.0 | all-reduce | flops 7 | bytes 56 | tf_op jit(solution)/shard_map/psum | solution.py:181
  583.1 2.5 multiply_subtract_fusion.5
  591.7 3.0 collective-permute-start.37
  597.5 5.1 collective-permute-start.39
  607.0 3.3 collective-permute-start.41
  612.4 5.2 collective-permute-start.43
  619.5 2.8 divide_subtract_fusion
  622.3 6.9 while.120
  629.5 70.3 %all_gather.34 = f32[32,2,512]{2,1,0:T(2,128)S(1)} all-gather(f32[1,2,512]{2,1,0:T(2,128)S(1)} %dynamic_update_slice.47), channel_id=1, replica_groups=mesh['gx'=4,'gy'=8] {'gx','gy'}, dimensions={0}, use_global_device_ids=true | all-gather | bytes 135168 | tf_op jit(solution)/shard_map/all_gather | solution.py:144
  701.4 4.3 while.116
  708.5 3.0 collective-permute-start.45
  713.7 4.5 collective-permute-start.47
  728.9 43.6 %all-reduce.26 = (f32[2,4]{0,1:T(4,128)S(1)}, f32[]{:T(128)}) all-reduce(f32[2,4]{0,1:T(4,128)S(1)} %pad_maximum_fusion.162, f32[]{:T(128)} %fusion.133), channel_id=1, replica_groups=mesh['gx'=4,'gy'=8] {'gx','gy'}, use_global_device_ids=true, to_apply=%region_54.0 | all-reduce | flops 9 | bytes 72 | tf_op jit(solution)/shard_map/psum | solution.py:181
  778.3 1.9 multiply_reduce_fusion.61
  782.2 2.0 fusion.293
  784.2 2.0 multiply_reduce_fusion.55
  786.2 1.9 multiply_reduce_fusion.57
  798.0 1.9 multiply_reduce_fusion.47
  801.2 2.6 multiply_reduce_fusion.41
  803.8 2.0 multiply_reduce_fusion.40
  807.6 2.6 multiply_reduce_fusion.39
  810.9 1.9 multiply_reduce_fusion.38
  812.8 2.0 fusion.299
  816.6 1.9 multiply_reduce_fusion.30
  818.5 3.1 multiply_reduce_fusion.29
  825.9 1.9 multiply_reduce_fusion.27
  829.1 2.6 multiply_reduce_fusion.19
  833.5 3.1 multiply_reduce_fusion.17
  841.5 2.6 multiply_reduce_fusion.15
  844.8 1.9 multiply_reduce_fusion.14
  851.2 2.0 multiply_reduce_fusion.11
  858.9 1.9 multiply_reduce_fusion.7
  (478 shorter events, 200.2 us)
Async XLA Ops:
  0.6 44.7 %copy-start.23 = (f32[2,16,32,128]{3,2,1,0:T(8,128)S(1)}, f32[2,16,32,128]{3,2,1,0:T(8,128)}, u32[]{:S(2)}) copy-start(f32[2,16,32,128]{3,2,1,0:T(8,128)} %param.23) | copy-start | bytes 1572868
  46.6 369.3 %copy-start.6 = (f32[16,32,128]{2,1,0:T(8,128)}, f32[16,32,128]{2,1,0:T(8,128)S(1)}, u32[]{:S(2)}) copy-start(f32[16,32,128]{2,1,0:T(8,128)S(1)} %get-tuple-element.1108) | copy-start | bytes 786436
  46.7 4.3 collective-permute-start
  48.0 3.9 collective-permute-start.1
  51.9 6.5 collective-permute-start.2
  53.2 6.5 collective-permute-start.3
  61.0 4.3 collective-permute-start.4
  62.3 3.9 collective-permute-start.5
  66.2 7.0 collective-permute-start.6
  67.5 6.9 collective-permute-start.7
  159.8 4.3 collective-permute-start.8
  161.1 3.9 collective-permute-start.9
  165.0 6.1 collective-permute-start.10
  166.3 6.0 collective-permute-start.11
  173.5 61.3 %copy-start.24 = (f32[16,32,128]{2,1,0:T(8,128)}, f32[16,32,128]{2,1,0:T(8,128)S(1)}, u32[]{:S(2)}) copy-start(f32[16,32,128]{2,1,0:T(8,128)S(1)} %get-tuple-element.1104) | copy-start | bytes 786436
  173.5 61.3 %copy-start.26 = (f32[16,32,128]{2,1,0:T(8,128)}, f32[16,32,128]{2,1,0:T(8,128)S(1)}, u32[]{:S(2)}) copy-start(f32[16,32,128]{2,1,0:T(8,128)S(1)} %get-tuple-element.1105) | copy-start | bytes 786436
  221.1 13.7 %copy-start.41 = (f32[1,16,32,128]{3,2,1,0:T(8,128)}, f32[1,16,32,128]{3,2,1,0:T(8,128)S(1)}, u32[]{:S(2)}) copy-start(f32[1,16,32,128]{3,2,1,0:T(8,128)S(1)} %get-tuple-element.1218) | copy-start | bytes 786436
  221.2 177.9 %copy-start.2 = (f32[2,16,32,128]{3,2,1,0:T(8,128)}, f32[2,16,32,128]{3,2,1,0:T(8,128)S(1)}, u32[]{:S(2)}) copy-start(f32[2,16,32,128]{3,2,1,0:T(8,128)S(1)} %fusion.124) | copy-start | bytes 1572868
  221.4 13.8 %copy-start.16 = (f32[16,32,128]{2,1,0:T(8,128)}, f32[16,32,128]{2,1,0:T(8,128)S(1)}, u32[]{:S(2)}) copy-start(f32[16,32,128]{2,1,0:T(8,128)S(1)} %get-tuple-element.1136) | copy-start | bytes 786436
  221.4 13.8 %copy-start.18 = (f32[16,32,128]{2,1,0:T(8,128)}, f32[16,32,128]{2,1,0:T(8,128)S(1)}, u32[]{:S(2)}) copy-start(f32[16,32,128]{2,1,0:T(8,128)S(1)} %get-tuple-element.1137) | copy-start | bytes 786436
  221.4 4.3 collective-permute-start.12
  222.7 3.9 collective-permute-start.13
  226.6 6.5 collective-permute-start.14
  227.9 6.4 collective-permute-start.15
  236.5 4.7 collective-permute-start.16
  237.8 4.5 collective-permute-start.17
  242.3 6.9 collective-permute-start.18
  243.6 6.6 collective-permute-start.19
  336.5 4.3 collective-permute-start.20
  337.8 3.9 collective-permute-start.21
  341.7 6.1 collective-permute-start.22
  343.0 6.0 collective-permute-start.23
  400.5 15.2 %copy-start.45 = (f32[1,16,32,128]{3,2,1,0:T(8,128)}, f32[1,16,32,128]{3,2,1,0:T(8,128)S(1)}, u32[]{:S(2)}) copy-start(f32[1,16,32,128]{3,2,1,0:T(8,128)S(1)} %get-tuple-element.1202) | copy-start | bytes 786436
  400.5 15.2 %copy-start.47 = (f32[1,16,32,128]{3,2,1,0:T(8,128)}, f32[1,16,32,128]{3,2,1,0:T(8,128)S(1)}, u32[]{:S(2)}) copy-start(f32[1,16,32,128]{3,2,1,0:T(8,128)S(1)} %get-tuple-element.1203) | copy-start | bytes 786436
  401.9 13.8 %copy-start.49 = (f32[1,16,32,128]{3,2,1,0:T(8,128)}, f32[1,16,32,128]{3,2,1,0:T(8,128)S(1)}, u32[]{:S(2)}) copy-start(f32[1,16,32,128]{3,2,1,0:T(8,128)S(1)} %get-tuple-element.1204) | copy-start | bytes 786436
  401.9 13.8 %copy-start.51 = (f32[1,16,32,128]{3,2,1,0:T(8,128)}, f32[1,16,32,128]{3,2,1,0:T(8,128)S(1)}, u32[]{:S(2)}) copy-start(f32[1,16,32,128]{3,2,1,0:T(8,128)S(1)} %get-tuple-element.1205) | copy-start | bytes 786436
  402.2 13.8 %copy-start.12 = (f32[16,32,128]{2,1,0:T(8,128)}, f32[16,32,128]{2,1,0:T(8,128)S(1)}, u32[]{:S(2)}) copy-start(f32[16,32,128]{2,1,0:T(8,128)S(1)} %get-tuple-element.1132) | copy-start | bytes 786436
  402.2 13.8 %copy-start.14 = (f32[16,32,128]{2,1,0:T(8,128)}, f32[16,32,128]{2,1,0:T(8,128)S(1)}, u32[]{:S(2)}) copy-start(f32[16,32,128]{2,1,0:T(8,128)S(1)} %get-tuple-element.1133) | copy-start | bytes 786436
  402.3 4.3 collective-permute-start.24
  403.6 3.9 collective-permute-start.25
  407.5 6.5 collective-permute-start.26
  408.8 6.4 collective-permute-start.27
  416.9 4.7 collective-permute-start.28
  418.2 4.3 collective-permute-start.29
  422.5 6.7 collective-permute-start.30
  423.8 6.6 collective-permute-start.31
  517.0 4.4 collective-permute-start.32
  518.3 3.9 collective-permute-start.33
  522.2 6.1 collective-permute-start.34
  523.5 6.0 collective-permute-start.35
  590.3 14.6 %copy-start.8 = (f32[16,32,128]{2,1,0:T(8,128)}, f32[16,32,128]{2,1,0:T(8,128)S(1)}, u32[]{:S(2)}) copy-start(f32[16,32,128]{2,1,0:T(8,128)S(1)} %get-tuple-element.1128) | copy-start | bytes 786436
  590.3 14.6 %copy-start.10 = (f32[16,32,128]{2,1,0:T(8,128)}, f32[16,32,128]{2,1,0:T(8,128)S(1)}, u32[]{:S(2)}) copy-start(f32[16,32,128]{2,1,0:T(8,128)S(1)} %get-tuple-element.1129) | copy-start | bytes 786436
  590.4 5.8 collective-permute-start.36
  591.7 4.5 collective-permute-start.37
  596.2 6.6 collective-permute-start.38
  597.5 6.5 collective-permute-start.39
  605.7 4.8 collective-permute-start.40
  607.0 4.1 collective-permute-start.41
  611.1 6.7 collective-permute-start.42
  612.4 6.6 collective-permute-start.43
  707.2 4.4 collective-permute-start.44
  708.5 3.9 collective-permute-start.45
  712.4 6.1 collective-permute-start.46
  713.7 6.0 collective-permute-start.47
  (52 other events, 79.5 us)
